TPU v7x, 256 devices: a whole 4x4x8 slice. The times are simulated.
256 devices in a mesh: gx: 4 (over x), gy: 4 (over y_lo, core), gz: 16 (over z, y_hi).
Axes of the slice: x: 4, y: 4 (y_hi: 2, y_lo: 2; y = y_hi * 2 + y_lo), z: 8, core: 2. Of those that a mesh axis runs over, the one named last changes fastest.
Arguments:
- left_modes: bfloat16 [2, 4, 2, 128, 3, 131072], P(None, None, None, None, None, ('gx', 'gy', 'gz')), may hold values from -0.14160156 to 0.14160156
- right_modes: bfloat16 [2, 4, 2, 128, 3, 131072], P(None, None, None, None, None, ('gx', 'gy', 'gz')), may hold values from -0.14160156 to 0.14160156
- gamma_cols: int32 [16, 4], replicated, may hold values from 0 to 3, each once within a row
- gamma_phase: int32 [16, 4], replicated, may hold values from 0 to 3
- dilution: int32 [64], replicated, may hold values from 0 to 3
- time_pairs: int32 [4, 2], replicated, may hold values from 0 to 1
Outputs:
- meson_fields: float32 [16, 2, 2, 128, 128], P('gz', None, None, ('gx', 'gy'))
- traces: float32 [4, 16, 16, 2], P(None, 'gz')
Inputs may be any that keep to these rules, and one draw needn't show every extreme that they name: Each row of gamma_cols is a permutation of the four spins.
All inputs are finite; a program needn't handle non-finite values.
Results may differ from a plain program's by a relative error of at most 0.0003.
Values sent between devices are 32-bit elements; how exact they have to be, the bound alone decides.
No kernel may reach another device: no remote copies, remote signals or barrier semaphores. Data moves between devices by JAX's collectives and lax.ppermute only.
A program may use at most 128 MiB of HBM per device.

v0:
```python
import jax
import jax.numpy as jnp
from jax import lax
from jax.sharding import PartitionSpec as P

EXACT = lax.Precision.HIGHEST


def coefficients(gamma_cols, gamma_phase):
    spin_ids = jnp.arange(4, dtype=jnp.int32)
    onehot = (gamma_cols[:, :, None] == spin_ids[None, None, :]).astype(jnp.float32)
    real_sign = (gamma_phase == 0).astype(jnp.float32) - (gamma_phase == 2).astype(jnp.float32)
    imag_sign = (gamma_phase == 1).astype(jnp.float32) - (gamma_phase == 3).astype(jnp.float32)
    return (onehot * real_sign[:, :, None], onehot * imag_sign[:, :, None])


def select_pairs(crossed, time_pairs):
    time_ids = jnp.arange(crossed.shape[1], dtype=jnp.int32)
    first_time = (time_pairs[:, 0:1] == time_ids[None, :]).astype(jnp.float32)
    second_time = (time_pairs[:, 1:2] == time_ids[None, :]).astype(jnp.float32)
    chosen = jnp.einsum("pt,pu,gtahub->pgahb", first_time, second_time, crossed, precision=EXACT)
    real_part = chosen[:, :, 0, :, 0] - chosen[:, :, 1, :, 1]
    imag_part = chosen[:, :, 0, :, 1] + chosen[:, :, 1, :, 0]
    return jnp.stack([real_part, imag_part], axis=-1)


def project(coef_re, coef_im, pair_re, pair_im, form, part_axis):
    meson_re = jnp.einsum(form, coef_re, pair_re, precision=EXACT) - jnp.einsum(
        form, coef_im, pair_im, precision=EXACT
    )
    meson_im = jnp.einsum(form, coef_re, pair_im, precision=EXACT) + jnp.einsum(
        form, coef_im, pair_re, precision=EXACT
    )
    return jnp.stack([meson_re, meson_im], axis=part_axis)


def finish_whole(summed, time_pairs, local_gammas, block_rows, mode_count):
    group_start = lax.axis_index("gz") * local_gammas
    my_gammas = lax.dynamic_slice_in_dim(summed, group_start, local_gammas, 0)
    row_block = lax.axis_index("gx") * lax.axis_size("gy") + lax.axis_index("gy")
    meson_fields = lax.dynamic_slice_in_dim(my_gammas, row_block * block_rows, block_rows, 3)
    crossed = jnp.einsum("gtaij,hubji->gtahub", my_gammas, summed, precision=EXACT)
    traces = select_pairs(crossed, time_pairs) / mode_count
    return (meson_fields, traces)


def local(left_modes, right_modes, gamma_cols, gamma_phase, dilution, time_pairs):
    times_held = left_modes.shape[0]
    mode_count = left_modes.shape[3]
    gamma_count = gamma_cols.shape[0]
    noise_count = dilution.shape[0]
    low_count = mode_count - noise_count
    coef_re, coef_im = coefficients(gamma_cols, gamma_phase)
    groups = lax.axis_size("gz")
    blocks = lax.axis_size("gx") * lax.axis_size("gy")
    local_gammas = gamma_count // groups
    block_rows = mode_count // blocks
    spin_ids = jnp.arange(4, dtype=jnp.int32)
    noise_onehot = dilution[None, :] == spin_ids[:, None]
    select_table = noise_onehot.astype(jnp.bfloat16)
    low_re_list = []
    low_im_list = []
    noise_re_list = []
    noise_im_list = []
    for time_slot in range(times_held):
        left_slot = left_modes[time_slot]
        right_slot = right_modes[time_slot]
        low_prod = jnp.einsum(
            "spicx,qrjcx->sqpirj",
            left_slot,
            right_slot[:, :, :low_count],
            preferred_element_type=jnp.float32,
        )
        noise_right = jnp.sum(
            right_slot[:, :, low_count:] * select_table[:, None, :, None, None], axis=0
        )
        noise_prod = jnp.einsum(
            "spicx,qjcx->spiqj", left_slot, noise_right, preferred_element_type=jnp.float32
        )
        low_re_list.append(low_prod[:, :, 0, :, 0, :] + low_prod[:, :, 1, :, 1, :])
        low_im_list.append(low_prod[:, :, 0, :, 1, :] - low_prod[:, :, 1, :, 0, :])
        noise_re_list.append(noise_prod[:, 0, :, 0, :] + noise_prod[:, 1, :, 1, :])
        noise_im_list.append(noise_prod[:, 0, :, 1, :] - noise_prod[:, 1, :, 0, :])
    low_re, low_im, noise_re, noise_im = lax.psum(
        (
            jnp.stack(low_re_list),
            jnp.stack(low_im_list),
            jnp.stack(noise_re_list),
            jnp.stack(noise_im_list),
        ),
        ("gx", "gy", "gz"),
    )
    noise_float = noise_onehot.astype(jnp.float32)
    noise_coef_re = jnp.einsum("gsr,rj->gsj", coef_re, noise_float, precision=EXACT)
    noise_coef_im = jnp.einsum("gsr,rj->gsj", coef_im, noise_float, precision=EXACT)
    low_part = project(coef_re, coef_im, low_re, low_im, "gsr,tsrij->gtij", 2)
    noise_part = project(noise_coef_re, noise_coef_im, noise_re, noise_im, "gsj,tsij->gtij", 2)
    summed = jnp.concatenate([low_part, noise_part], axis=4)
    meson_fields, traces = finish_whole(summed, time_pairs, local_gammas, block_rows, mode_count)
    return (meson_fields, traces)


def solution(mesh):
    return jax.shard_map(
        local,
        mesh=mesh,
        in_specs=(
            P(None, None, None, None, None, ("gx", "gy", "gz")),
            P(None, None, None, None, None, ("gx", "gy", "gz")),
            P(),
            P(),
            P(),
            P(),
        ),
        out_specs=(P("gz", None, None, ("gx", "gy"), None), P(None, "gz", None, None)),
        check_vma=False,
    )
```

profile of v0, /device:TPU:2, one launch (start us, length us, event | category | flops | bytes accessed | tf_op | source)
XLA Modules:
  0.0 340.3 jit_solution(10529417758410979270)
XLA Ops:
  7.2 3.5 %slice_bitcast_fusion = (bf16[4,2,128,3,512]{4,2,3,1,0:T(8,128)(2,1)S(1)}, bf16[4,2,128,3,512]{4,2,3,1,0:T(8,128)(2,1)S(1)}) fusion(bf16[2,4,2,128,3,512]{5,3,4,2,1,0:T(8,128)(2,1)} %param.7), kind=kLoop, calls=%fused_computation.11 | loop fusion | bytes 12582912 | tf_op jit(solution)/shard_map/squeeze | solution.py:67
  10.7 1.1 copy-done.3
  11.9 0.7 slice_bitcast_fusion.3
  12.6 0.9 fusion.19
  13.5 1.1 fusion.30
  14.7 1.8 fusion.15
  16.7 1.1 fusion.27
  17.8 1.8 fusion.12
  19.8 0.8 pad_maximum_fusion.2
  20.6 1.5 pad_maximum_fusion
  22.9 268.4 %all-reduce.3.cloned.1.call-done = (f32[2,4,128,64]{2,3,1,0:T(8,128)}, f32[2,4,128,64]{2,3,1,0:T(8,128)}, f32[2,4,4,128,64]{3,4,1,2,0:T(8,128)}, f32[2,4,4,128,64]{3,4,1,2,0:T(8,128)}) async-done(((f32[2,4,128,64]{2,3,1,0:T(8,128)}, f32[2,4,128,64]{2,3,1,0:T(8,128)}, f32[2,4,4,128,64]{3,4,1,2,0:T(8,128)}, f32[2,4,4,128,64]{3,4,1,2,0:T(8,128)}), (f32[2,4,128,64]{2,3,1,0:T(8,128)}, ...) | async-done | bytes 2621456 | tf_op jit(solution)/shard_map/psum | solution.py:84
  291.3 3.3 convolution_bitcast_fusion.2
  294.6 3.3 convolution_bitcast_fusion
  298.0 2.0 fusion.24
  300.0 2.2 fusion.26
  302.2 1.2 fusion.48
  303.4 1.2 fusion.44
  304.5 1.2 fusion.22
  305.7 1.2 fusion.21
  306.9 2.7 fusion.101
  309.6 2.0 copy-done
  311.9 17.7 %fusion = f32[2,2,16,2,2,1]{2,1,5,4,3,0:T(2,128)S(1)} fusion(f32[2,2,128,128,1,1]{3,1,2,5,4,0:T(2,128)S(1)} %copy.67, f32[16,2,2,128,128,1]{3,0,4,1,2,5:T(8,128)} %get-tuple-element.14), kind=kOutput, calls=%fused_computation.1 | convolution fusion | flops 50331648 | bytes 4457472 | tf_op jit(solution)/shard_map/gtaij,hubji->gtahub/dot_general | solution.py:42
  330.5 2.2 constant_dynamic-slice_fusion.1
  332.7 0.7 copy.34
  (40 shorter events, 2.2 us)
Async XLA Ops:
  7.2 3.6 %copy-start.7 = (s32[64]{0:T(128)S(1)}, s32[64]{0:T(128)}, u32[]{:S(2)}) copy-start(s32[64]{0:T(128)} %param.10) | copy-start | bytes 772
  7.2 284.1 %all-reduce.3.cloned.1.call-start = ((), (), s32[]{:S(2)}) async-start(), calls=%async_computation | async-start | bytes 5242880 | tf_op jit(solution)/shard_map/psum | solution.py:84
  7.2 4.6 %copy-start.3 = (bf16[2,4,2,128,3,512]{5,3,4,2,1,0:T(8,128)(2,1)S(1)}, bf16[2,4,2,128,3,512]{5,3,4,2,1,0:T(8,128)(2,1)}, u32[]{:S(2)}) copy-start(bf16[2,4,2,128,3,512]{5,3,4,2,1,0:T(8,128)(2,1)} %param.6) | copy-start | bytes 18874372
  20.6 1.5 copy-start.8
  20.6 1.6 copy-start.6
  20.6 2.3 copy-start.9
  291.3 6.6 %copy-start.2 = (f32[2,4,4,128,64]{3,4,1,2,0:T(8,128)S(1)}, f32[2,4,4,128,64]{3,4,1,2,0:T(8,128)}, u32[]{:S(2)}) copy-start(f32[2,4,4,128,64]{3,4,1,2,0:T(8,128)} %get-tuple-element.8) | copy-start | bytes 3145732
  294.6 5.4 %copy-start.1 = (f32[2,4,4,128,64]{3,4,1,2,0:T(8,128)S(1)}, f32[2,4,4,128,64]{3,4,1,2,0:T(8,128)}, u32[]{:S(2)}) copy-start(f32[2,4,4,128,64]{3,4,1,2,0:T(8,128)} %get-tuple-element.9) | copy-start | bytes 3145732
  298.0 4.2 %copy-start.4 = (f32[2,4,128,64]{2,3,1,0:T(8,128)S(1)}, f32[2,4,128,64]{2,3,1,0:T(8,128)}, u32[]{:S(2)}) copy-start(f32[2,4,128,64]{2,3,1,0:T(8,128)} %get-tuple-element.7) | copy-start | bytes 786436
  298.0 5.4 %copy-start.5 = (f32[2,4,128,64]{2,3,1,0:T(8,128)S(1)}, f32[2,4,128,64]{2,3,1,0:T(8,128)}, u32[]{:S(2)}) copy-start(f32[2,4,128,64]{2,3,1,0:T(8,128)} %get-tuple-element.6) | copy-start | bytes 786436
  309.6 2.0 copy-start
Sparse Core Ops, SparseCore 0:
  22.3 268.9 all-reduce.2
where the time goes:
time: 340 us
  waiting for transfers between devices  268 us (79%)
  matrix products  39.7 us (12%)
  between operations  14.4 us (4%)
  local copies, waits for them, and re-layouts  11.4 us (3%)
  other arithmetic  6.28 us (2%)
    psum x1, waiting for transfers between devices, local(): lax.psum((jnp.stack(low_re_list), jnp.stack(low_im_list), jnp.stack(noise...  268 us
    dot_general x1, matrix products, finish_whole(): jnp.einsum('gtaij,hubji->gtahub', my_gammas, summed, precision=EXACT)  17.7 us
  transfers between devices with their start and end apart: 1, of which 1 were waited for; matrix products, arithmetic and copies ran while one was open for 0% of the time, Pallas kernels for 0%

commit v1 on v0

--- a/solution.py
+++ b/solution.py
@@ -82,13 +82,16 @@
         noise_re_list.append(noise_prod[:, 0, :, 0, :] + noise_prod[:, 1, :, 1, :])
         noise_im_list.append(noise_prod[:, 0, :, 1, :] - noise_prod[:, 1, :, 0, :])
     low_re, low_im, noise_re, noise_im = lax.psum(
-        (
-            jnp.stack(low_re_list),
-            jnp.stack(low_im_list),
-            jnp.stack(noise_re_list),
-            jnp.stack(noise_im_list),
+        lax.psum(
+            (
+                jnp.stack(low_re_list),
+                jnp.stack(low_im_list),
+                jnp.stack(noise_re_list),
+                jnp.stack(noise_im_list),
+            ),
+            ("gy", "gz"),
         ),
-        ("gx", "gy", "gz"),
+        "gx",
     )
     noise_float = noise_onehot.astype(jnp.float32)
     noise_coef_re = jnp.einsum("gsr,rj->gsj", coef_re, noise_float, precision=EXACT)

time: 340 us -> 341 us (level)
    psum x1, waiting for transfers between devices: 268 us -> 195 us  [local(): lax.psum((jnp.stack(low_re_list), jnp.stack(low_im_list), jnp.stack(noise...]
    psum x0 -> x1, waiting for transfers between devices: none -> 71.7 us  [local(): lax.psum(lax.psum((jnp.stack(low_re_list), jnp.stack(low_im_list), jnp.st...]
  transfers between devices with their start and end apart: 1 -> 2, of which waited for: 1 -> 2; matrix products, arithmetic and copies ran while one was open for 0% -> 0% of each run, Pallas kernels for 0% -> 0%
where the time goes in v1:
time: 341 us; the launch traced here: 339 us
  waiting for transfers between devices  267 us (78%)
  matrix products  39.5 us (12%)
  between operations  14.4 us (4%)
  local copies, waits for them, and re-layouts  11.4 us (3%)
  other arithmetic  6.25 us (2%)
    psum x1, waiting for transfers between devices, local(): lax.psum((jnp.stack(low_re_list), jnp.stack(low_im_list), jnp.stack(noise...  195 us
    psum x1, waiting for transfers between devices, local(): lax.psum(lax.psum((jnp.stack(low_re_list), jnp.stack(low_im_list), jnp.st...  71.7 us
    dot_general x1, matrix products, finish_whole(): jnp.einsum('gtaij,hubji->gtahub', my_gammas, summed, precision=EXACT)  17.5 us
  transfers between devices with their start and end apart: 2, of which 2 were waited for; matrix products, arithmetic and copies ran while one was open for 0% of the time, Pallas kernels for 0%

profile of v1, /device:TPU:2, one launch (start us, length us, event | category | flops | bytes accessed | tf_op | source)
XLA Modules:
  0.0 338.8 jit_solution(16233469823831601025)
XLA Ops:
  7.2 3.5 %slice_bitcast_fusion = (bf16[4,2,128,3,512]{4,2,3,1,0:T(8,128)(2,1)S(1)}, bf16[4,2,128,3,512]{4,2,3,1,0:T(8,128)(2,1)S(1)}) fusion(bf16[2,4,2,128,3,512]{5,3,4,2,1,0:T(8,128)(2,1)} %param.7), kind=kLoop, calls=%fused_computation.11 | loop fusion | bytes 12582912 | tf_op jit(solution)/shard_map/squeeze | solution.py:67
  10.7 1.1 copy-done.3
  11.9 0.7 slice_bitcast_fusion.3
  12.6 0.9 fusion.19
  13.5 1.1 fusion.30
  14.7 1.8 fusion.15
  16.7 1.1 fusion.27
  17.8 1.8 fusion.12
  19.8 0.8 pad_maximum_fusion.2
  20.6 1.5 pad_maximum_fusion
  22.4 195.1 %all-reduce.5.cloned.1.call-done = (f32[2,4,128,64]{2,3,1,0:T(8,128)}, f32[2,4,128,64]{2,3,1,0:T(8,128)}, f32[2,4,4,128,64]{3,4,1,2,0:T(8,128)}, f32[2,4,4,128,64]{3,4,1,2,0:T(8,128)}) async-done(((f32[2,4,128,64]{2,3,1,0:T(8,128)}, f32[2,4,128,64]{2,3,1,0:T(8,128)}, f32[2,4,4,128,64]{3,4,1,2,0:T(8,128)}, f32[2,4,4,128,64]{3,4,1,2,0:T(8,128)}), (f32[2,4,128,64]{2,3,1,0:T(8,128)}, ...) | async-done | bytes 2621456 | tf_op jit(solution)/shard_map/psum | solution.py:85
  218.3 71.7 %all-reduce.7.cloned.1.call-done = (f32[2,4,128,64]{2,3,1,0:T(8,128)}, f32[2,4,128,64]{2,3,1,0:T(8,128)}, f32[2,4,4,128,64]{3,4,1,2,0:T(8,128)}, f32[2,4,4,128,64]{3,4,1,2,0:T(8,128)}) async-done(((f32[2,4,128,64]{2,3,1,0:T(8,128)}, f32[2,4,128,64]{2,3,1,0:T(8,128)}, f32[2,4,4,128,64]{3,4,1,2,0:T(8,128)}, f32[2,4,4,128,64]{3,4,1,2,0:T(8,128)}), (f32[2,4,128,64]{2,3,1,0:T(8,128)}, ...) | async-done | bytes 2621456 | tf_op jit(solution)/shard_map/psum | solution.py:84
  290.0 3.3 convolution_bitcast_fusion.2
  293.3 3.3 convolution_bitcast_fusion
  296.7 2.0 fusion.24
  298.7 2.0 fusion.26
  300.7 1.2 fusion.48
  301.9 1.2 fusion.44
  303.1 1.2 fusion.22
  304.2 1.4 fusion.21
  305.6 2.7 fusion.101
  308.3 2.0 copy-done
  310.7 17.5 %fusion = f32[2,2,16,2,2,1]{2,1,5,4,3,0:T(2,128)S(1)} fusion(f32[2,2,128,128,1,1]{3,1,2,5,4,0:T(2,128)S(1)} %copy.67, f32[16,2,2,128,128,1]{3,0,4,1,2,5:T(8,128)} %get-tuple-element.18), kind=kOutput, calls=%fused_computation.1 | convolution fusion | flops 50331648 | bytes 4457472 | tf_op jit(solution)/shard_map/gtaij,hubji->gtahub/dot_general | solution.py:42
  329.0 2.2 constant_dynamic-slice_fusion.1
  (43 shorter events, 3.2 us)
Async XLA Ops:
  7.2 3.6 %copy-start.7 = (s32[64]{0:T(128)S(1)}, s32[64]{0:T(128)}, u32[]{:S(2)}) copy-start(s32[64]{0:T(128)} %param.10) | copy-start | bytes 772
  7.2 210.4 %all-reduce.5.cloned.1.call-start = ((), (), s32[]{:S(2)}) async-start(), calls=%async_computation | async-start | bytes 5242880 | tf_op jit(solution)/shard_map/psum | solution.py:85
  7.2 4.6 %copy-start.3 = (bf16[2,4,2,128,3,512]{5,3,4,2,1,0:T(8,128)(2,1)S(1)}, bf16[2,4,2,128,3,512]{5,3,4,2,1,0:T(8,128)(2,1)}, u32[]{:S(2)}) copy-start(bf16[2,4,2,128,3,512]{5,3,4,2,1,0:T(8,128)(2,1)} %param.6) | copy-start | bytes 18874372
  22.1 195.4 %copy-start.8 = (s32[16,4]{0,1:T(4,128)S(1)}, s32[16,4]{0,1:T(4,128)}, u32[]{:S(2)}) copy-start(s32[16,4]{0,1:T(4,128)} %param.9) | copy-start | bytes 772
  22.1 195.5 %copy-start.6 = (s32[16,4]{0,1:T(4,128)S(1)}, s32[16,4]{0,1:T(4,128)}, u32[]{:S(2)}) copy-start(s32[16,4]{0,1:T(4,128)} %param.8) | copy-start | bytes 772
  22.1 196.1 %copy-start.9 = (s32[4,2]{0,1:T(2,128)S(1)}, s32[4,2]{0,1:T(2,128)}, u32[]{:S(2)}) copy-start(s32[4,2]{0,1:T(2,128)} %param.11) | copy-start | bytes 100
  22.2 267.9 %all-reduce.7.cloned.1.call-start = ((), (), s32[]{:S(2)}) async-start(), calls=%async_computation.1 | async-start | bytes 5242880 | tf_op jit(solution)/shard_map/psum | solution.py:84
  290.0 6.6 %copy-start.2 = (f32[2,4,4,128,64]{3,4,1,2,0:T(8,128)S(1)}, f32[2,4,4,128,64]{3,4,1,2,0:T(8,128)}, u32[]{:S(2)}) copy-start(f32[2,4,4,128,64]{3,4,1,2,0:T(8,128)} %get-tuple-element.12) | copy-start | bytes 3145732
  293.3 5.4 %copy-start.1 = (f32[2,4,4,128,64]{3,4,1,2,0:T(8,128)S(1)}, f32[2,4,4,128,64]{3,4,1,2,0:T(8,128)}, u32[]{:S(2)}) copy-start(f32[2,4,4,128,64]{3,4,1,2,0:T(8,128)} %get-tuple-element.13) | copy-start | bytes 3145732
  296.7 4.0 %copy-start.4 = (f32[2,4,128,64]{2,3,1,0:T(8,128)S(1)}, f32[2,4,128,64]{2,3,1,0:T(8,128)}, u32[]{:S(2)}) copy-start(f32[2,4,128,64]{2,3,1,0:T(8,128)} %get-tuple-element.11) | copy-start | bytes 786436
  296.7 5.2 %copy-start.5 = (f32[2,4,128,64]{2,3,1,0:T(8,128)S(1)}, f32[2,4,128,64]{2,3,1,0:T(8,128)}, u32[]{:S(2)}) copy-start(f32[2,4,128,64]{2,3,1,0:T(8,128)} %get-tuple-element.10) | copy-start | bytes 786436
  308.3 2.0 copy-start
Sparse Core Ops, SparseCore 0:
  22.3 195.2 all-reduce.4
  220.1 69.8 all-reduce.6
